TPU v7x, 32 devices: a whole 2x2x4 slice. The times are simulated.
32 devices in a mesh: aux: 16 (over z, y, x), ao: 2 (over core).
Axes of the slice: x: 2, y: 2, z: 4, core: 2. Of those that a mesh axis runs over, the one named last changes fastest.
Arguments:
- ints: bfloat16 [256, 768, 768], P('aux', 'ao'), may hold values from -1.25 to 1.25
- occ_coef: bfloat16 [768, 32], replicated, may hold values from -0.21875 to 0.21875
- vir_coef: bfloat16 [768, 512], P('ao'), may hold values from -0.21875 to 0.21875
- occ_energy: float32 [32], replicated, may hold values from -2 to -0.3
- vir_energy: float32 [512], replicated, may hold values from 0.3 to 3
Outputs:
- density: float32 [32, 512, 512], P('aux', 'ao')
All inputs are finite; a program needn't handle non-finite values.
Results may differ from a plain program's by a relative error of at most 0.0065.
Values may be sent and summed in bfloat16 or wider, within the bound.
A program may use at most 128 MiB of HBM per device.

v0:
```python
import jax
import jax.numpy as jnp
from jax import lax
from jax.sharding import PartitionSpec as P

CYCLE = 4


def passed_along(block, axis, distance):
    devices = range(lax.axis_size(axis))
    route = [((i - distance) % len(devices), i) for i in devices]
    return lax.ppermute(block, axis, route)


def shards(ints, occ_coef, vir_coef, occ_energy, vir_energy):
    aux_index = lax.axis_index("aux")
    ao_index = lax.axis_index("ao")
    aux_count = lax.axis_size("aux")
    ao_count = lax.axis_size("ao")
    occ_block = occ_coef.shape[1] // aux_count
    occ_share = occ_block // ao_count
    half_ints = jnp.einsum(
        "qmn,ni->qmi", ints, occ_coef, preferred_element_type=jnp.float32
    ).astype(jnp.bfloat16)
    partial_sum = jnp.einsum("qmi,ma->qia", half_ints, vir_coef, preferred_element_type=jnp.float32)
    summed_half = lax.psum_scatter(partial_sum, "ao", scatter_dimension=2, tiled=True).astype(
        jnp.bfloat16
    )
    grouped = lax.all_to_all(summed_half, "aux", split_axis=1, concat_axis=0, tiled=True)
    own_block = lax.all_gather(grouped, "ao", axis=2, tiled=True)
    own_energy = lax.dynamic_slice_in_dim(occ_energy, aux_index * occ_block, occ_block)
    pair_piece = lax.dynamic_slice_in_dim(own_block, ao_index * occ_share, occ_share, 1)
    vir_pairs = vir_energy[:, None] + vir_energy[None, :]
    nvir_full = own_block.shape[2]

    def add_pairs(density_sum, visitor, block_index):
        pair_energy = lax.dynamic_slice_in_dim(
            occ_energy, block_index * occ_block + ao_index * occ_share, occ_share
        )
        integrals = jnp.einsum(
            "qia,qjb->ijab", own_block, visitor, preferred_element_type=jnp.float32
        )
        energy_gap = (
            own_energy[:, None, None, None]
            + pair_energy[None, :, None, None]
            - vir_pairs[None, None]
        )
        scaled = integrals / energy_gap
        amplitude = scaled.astype(jnp.bfloat16)
        mixed = (2.0 * scaled - jnp.swapaxes(scaled, 2, 3)).astype(jnp.bfloat16)
        return density_sum + jnp.einsum(
            "ijac,ijbc->iab", amplitude, mixed, preferred_element_type=jnp.float32
        )

    density_start = jnp.zeros((occ_block, nvir_full, nvir_full), jnp.float32)
    density_sum = add_pairs(density_start, pair_piece, aux_index)
    from_below = pair_piece
    from_above = pair_piece
    for offset in range(1, CYCLE + 1):
        from_below = passed_along(from_below, "aux", 1)
        from_above = passed_along(from_above, "aux", -1)
        density_sum = add_pairs(
            density_sum, from_below, (aux_index + aux_count - offset) % aux_count
        )
        density_sum = add_pairs(density_sum, from_above, (aux_index + offset) % aux_count)
    return lax.psum_scatter(density_sum, "ao", scatter_dimension=1, tiled=True)


def solution(mesh):
    return jax.shard_map(
        shards,
        mesh=mesh,
        in_specs=(P("aux", "ao", None), P(), P("ao", None), P(), P()),
        out_specs=P("aux", "ao", None),
        check_vma=False,
    )
```

profile of v0, /device:TPU:0, one launch (start us, length us, event | category | flops | bytes accessed | tf_op | source)
XLA Modules:
  0.0 162.6 jit_solution(14696118252836336197)
XLA Ops:
  6.5 1.0 copy-done
  7.5 7.8 %fusion.9 = f32[16,32,512]{2,1,0:T(8,128)} fusion(bf16[16,384,768]{2,1,0:T(8,128)(2,1)} %param.5, bf16[384,512]{1,0:T(8,128)(2,1)S(1)} %copy-done, bf16[768,32]{0,1:T(8,128)(2,1)} %param.6), kind=kOutput, calls=%fused_computation.29 | convolution fusion | flops 503513088 | bytes 10928128 | tf_op jit(solution)/shard_map/qmi,ma->qia/dot_general | solution.py:25
  15.5 0.7 fusion.84
  16.2 10.4 %reduce-scatter.3.cloned.1.call-done = f32[16,32,256]{2,1,0:T(8,128)} async-done(((f32[16,32,512]{2,1,0:T(8,128)}), f32[16,32,256]{2,1,0:T(8,128)}) %reduce-scatter.3.cloned.1.call-update) | async-done | bytes 524304 | tf_op jit(solution)/shard_map/reduce_scatter | solution.py:26
  26.6 1.1 convert_element_type.61
  27.7 0.9 copy.61
  28.6 6.8 %all-to-all-start = ((bf16[16,32,256]{2,0,1:T(8,128)(2,1)}), bf16[16,32,256]{2,0,1:T(8,128)(2,1)S(1)}, u32[]{:S(2)}, u32[]{:S(2)}) async-start(bf16[16,32,256]{2,0,1:T(8,128)(2,1)} %copy.61), calls=%async_computation.1 | async-start | bytes 524288 | tf_op jit(solution)/shard_map/all_to_all | solution.py:29
  35.4 0.7 broadcast_add_fusion.1
  36.1 5.0 %broadcast_add_fusion.8 = (f32[2]{0:T(128)S(1)}, f32[2]{0:T(128)S(1)}, f32[2]{0:T(128)S(1)}, f32[2]{0:T(128)S(1)}, f32[2]{0:T(128)S(1)}, /*index=5*/f32[2]{0:T(128)S(1)}, f32[2]{0:T(128)S(1)}, f32[2]{0:T(128)S(1)}) fusion(f32[2]{0:T(128)S(1)} %get-tuple-element.6, f32[]{:T(128)} %bitcast.17, f32[]{:T(128)} %bitcast.65, f32[]{:T(128)} %bitcast.57, ...), kind=kLoop, calls=%fused_computation.93 | loop fusion | flops 16 | bytes 104 | tf_op jit(solution)/shard_map/add | solution.py:44
  41.1 1.1 broadcast_add_fusion
  42.2 3.5 %all-to-all-done = bf16[16,32,256]{2,0,1:T(8,128)(2,1)S(1)} async-done(((bf16[16,32,256]{2,0,1:T(8,128)(2,1)}), bf16[16,32,256]{2,0,1:T(8,128)(2,1)S(1)}, u32[]{:S(2)}, u32[]{:S(2)}) %all-to-all-start) | async-done | bytes 262176 | tf_op jit(solution)/shard_map/all_to_all | solution.py:29
  45.7 2.2 %all_gather.3 = bf16[256,2,512]{2,0,1:T(8,128)(2,1)S(1)} all-gather(bf16[256,2,256]{2,0,1:T(8,128)(2,1)S(1)} %bitcast.228), channel_id=1, replica_groups=mesh['aux'=16,'ao'=2] {'ao'}, dimensions={2}, use_global_device_ids=true | all-gather | bytes 786432 | tf_op jit(solution)/shard_map/all_gather | solution.py:30
  47.9 0.8 collective-permute-start
  48.7 4.9 %collective-permute-start.1 = (bf16[256,1,512]{2,0,1:T(8,128)(2,1)S(1)}, bf16[256,1,512]{2,0,1:T(8,128)(2,1)S(1)}, u32[]{:S(2)}, u32[]{:S(2)}) collective-permute-start(bf16[256,1,512]{2,0,1:T(8,128)(2,1)S(1)} %constant_dynamic-slice_fusion), channel_id=1, source_target_pairs={{2,0},{4,2},{6,4},{8,6},{10,8},{12,10},{14,12},{16,14},{18,16},{20... | collective-permute-start | bytes 786440 | tf_op jit(solution)/shard_map/ppermute | solution.py:12
  53.6 1.7 %bitcast_divide_fusion.8 = f32[2,1,512,512]{2,3,0,1:T(8,128)S(1)} fusion(bf16[256,2,512]{2,0,1:T(8,128)(2,1)S(1)} %all_gather.3, f32[512,512]{0,1:T(8,128)} %broadcast_add_fusion, f32[2]{0:T(128)S(1)} %get-tuple-element.14, bf16[256,1,512]{2,0,1:T(8,128)(2,1)S(1)} %constant_dynamic-slice_fusion), kind=kOutput, calls=%fused_computation.8 | convolution fusion | flops 269484032 | bytes 3932168 | tf_op jit(solution)/shard_map/qia,qjb->ijab/dot_general | solution.py:40
  55.3 1.8 %copy.64 = f32[2,1,512,512]{3,2,0,1:T(8,128)} copy(f32[2,1,512,512]{2,3,0,1:T(8,128)S(1)} %bitcast_divide_fusion.8) | data formatting | bytes 4194304 | tf_op jit(solution)/shard_map/div | solution.py:48
  57.1 3.9 %fusion.11 = f32[2,512,512]{2,1,0:T(8,128)} fusion(f32[2,1,512,512]{2,3,0,1:T(8,128)S(1)} %bitcast_divide_fusion.8, f32[2,1,512,512]{3,2,0,1:T(8,128)} %copy.64), kind=kOutput, calls=%fused_computation.31 | convolution fusion | flops 538968064 | bytes 6291456 | tf_op jit(solution)/shard_map/ijac,ijbc->iab/dot_general | solution.py:51
  61.0 1.3 collective-permute-done.1
  62.8 1.9 %copy.70 = f32[2,1,512,512]{3,2,0,1:T(8,128)} copy(f32[2,1,512,512]{2,3,0,1:T(8,128)S(1)} %bitcast_divide_fusion.6) | data formatting | bytes 4194304 | tf_op jit(solution)/shard_map/div | solution.py:48
  64.6 3.9 %fusion.17 = f32[2,512,512]{2,1,0:T(8,128)} fusion(f32[2,1,512,512]{2,3,0,1:T(8,128)S(1)} %bitcast_divide_fusion.6, f32[2,1,512,512]{3,2,0,1:T(8,128)} %copy.70), kind=kOutput, calls=%fused_computation.35 | convolution fusion | flops 538968064 | bytes 6291456 | tf_op jit(solution)/shard_map/ijac,ijbc->iab/dot_general | solution.py:51
  68.5 0.5 bitcast_divide_fusion.7
  69.0 1.9 %copy.67 = f32[2,1,512,512]{3,2,0,1:T(8,128)} copy(f32[2,1,512,512]{2,3,0,1:T(8,128)S(1)} %bitcast_divide_fusion.7) | data formatting | bytes 4194304 | tf_op jit(solution)/shard_map/div | solution.py:48
  70.9 0.6 collective-permute-start.2
  71.5 5.1 %collective-permute-start.3 = (bf16[256,1,512]{2,0,1:T(8,128)(2,1)S(1)}, bf16[256,1,512]{2,0,1:T(8,128)(2,1)S(1)}, u32[]{:S(2)}, u32[]{:S(2)}) collective-permute-start(bf16[256,1,512]{2,0,1:T(8,128)(2,1)S(1)} %collective-permute-done.1), channel_id=1, source_target_pairs={{2,0},{4,2},{6,4},{8,6},{10,8},{12,10},{14,12},{16,14},{18,16},{20... | collective-permute-start | bytes 786440 | tf_op jit(solution)/shard_map/ppermute | solution.py:12
  76.5 3.9 %fusion.14 = f32[2,512,512]{2,1,0:T(8,128)} fusion(f32[2,1,512,512]{2,3,0,1:T(8,128)S(1)} %bitcast_divide_fusion.7, f32[2,1,512,512]{3,2,0,1:T(8,128)} %copy.67), kind=kOutput, calls=%fused_computation.33 | convolution fusion | flops 538968064 | bytes 6291456 | tf_op jit(solution)/shard_map/ijac,ijbc->iab/dot_general | solution.py:51
  80.4 4.7 %collective-permute-done.3 = bf16[256,1,512]{2,0,1:T(8,128)(2,1)S(1)} collective-permute-done((bf16[256,1,512]{2,0,1:T(8,128)(2,1)S(1)}, bf16[256,1,512]{2,0,1:T(8,128)(2,1)S(1)}, u32[]{:S(2)}, u32[]{:S(2)}) %collective-permute-start.3) | collective-permute-done | bytes 262176 | tf_op jit(solution)/shard_map/ppermute | solution.py:12
  85.1 0.7 copy-done.12
  85.8 0.5 bitcast_divide_fusion.4
  86.3 1.9 %copy.76 = f32[2,1,512,512]{3,2,0,1:T(8,128)} copy(f32[2,1,512,512]{2,3,0,1:T(8,128)S(1)} %bitcast_divide_fusion.4) | data formatting | bytes 4194304 | tf_op jit(solution)/shard_map/div | solution.py:48
  88.2 4.0 %fusion.23 = f32[2,512,512]{2,1,0:T(8,128)} fusion(f32[2,1,512,512]{2,3,0,1:T(8,128)S(1)} %bitcast_divide_fusion.4, f32[2,1,512,512]{3,2,0,1:T(8,128)} %copy.76), kind=kOutput, calls=%fused_computation.39 | convolution fusion | flops 538968064 | bytes 6291456 | tf_op jit(solution)/shard_map/ijac,ijbc->iab/dot_general | solution.py:51
  92.2 0.5 bitcast_divide_fusion.5
  92.7 1.8 %copy.73 = f32[2,1,512,512]{3,2,0,1:T(8,128)} copy(f32[2,1,512,512]{2,3,0,1:T(8,128)S(1)} %bitcast_divide_fusion.5) | data formatting | bytes 4194304 | tf_op jit(solution)/shard_map/div | solution.py:48
  94.8 5.3 %collective-permute-start.5 = (bf16[256,1,512]{2,0,1:T(8,128)(2,1)}, bf16[256,1,512]{2,0,1:T(8,128)(2,1)S(1)}, u32[]{:S(2)}, u32[]{:S(2)}) collective-permute-start(bf16[256,1,512]{2,0,1:T(8,128)(2,1)} %copy-done.12), channel_id=1, source_target_pairs={{2,0},{4,2},{6,4},{8,6},{10,8},{12,10},{14,12},{16,14},{18,16},{20... | collective-permute-start | bytes 786440 | tf_op jit(solution)/shard_map/ppermute | solution.py:12
  100.1 3.9 %fusion.20 = f32[2,512,512]{2,1,0:T(8,128)} fusion(f32[2,1,512,512]{2,3,0,1:T(8,128)S(1)} %bitcast_divide_fusion.5, f32[2,1,512,512]{3,2,0,1:T(8,128)} %copy.73), kind=kOutput, calls=%fused_computation.37 | convolution fusion | flops 538968064 | bytes 6291456 | tf_op jit(solution)/shard_map/ijac,ijbc->iab/dot_general | solution.py:51
  104.0 2.9 %collective-permute-done.5 = bf16[256,1,512]{2,0,1:T(8,128)(2,1)S(1)} collective-permute-done((bf16[256,1,512]{2,0,1:T(8,128)(2,1)}, bf16[256,1,512]{2,0,1:T(8,128)(2,1)S(1)}, u32[]{:S(2)}, u32[]{:S(2)}) %collective-permute-start.5) | collective-permute-done | bytes 262176 | tf_op jit(solution)/shard_map/ppermute | solution.py:12
  107.4 1.8 %copy.82 = f32[2,1,512,512]{3,2,0,1:T(8,128)} copy(f32[2,1,512,512]{2,3,0,1:T(8,128)S(1)} %bitcast_divide_fusion.2) | data formatting | bytes 4194304 | tf_op jit(solution)/shard_map/div | solution.py:48
  109.2 3.9 %fusion.29 = f32[2,512,512]{2,1,0:T(8,128)} fusion(f32[2,1,512,512]{2,3,0,1:T(8,128)S(1)} %bitcast_divide_fusion.2, f32[2,1,512,512]{3,2,0,1:T(8,128)} %copy.82), kind=kOutput, calls=%fused_computation.43 | convolution fusion | flops 538968064 | bytes 6291456 | tf_op jit(solution)/shard_map/ijac,ijbc->iab/dot_general | solution.py:51
  113.2 0.5 bitcast_divide_fusion.3
  113.6 1.8 %copy.79 = f32[2,1,512,512]{3,2,0,1:T(8,128)} copy(f32[2,1,512,512]{2,3,0,1:T(8,128)S(1)} %bitcast_divide_fusion.3) | data formatting | bytes 4194304 | tf_op jit(solution)/shard_map/div | solution.py:48
  115.8 5.3 %collective-permute-start.7 = (bf16[256,1,512]{2,0,1:T(8,128)(2,1)S(1)}, bf16[256,1,512]{2,0,1:T(8,128)(2,1)S(1)}, u32[]{:S(2)}, u32[]{:S(2)}) collective-permute-start(bf16[256,1,512]{2,0,1:T(8,128)(2,1)S(1)} %collective-permute-done.5), channel_id=1, source_target_pairs={{2,0},{4,2},{6,4},{8,6},{10,8},{12,10},{14,12},{16,14},{18,16},{20... | collective-permute-start | bytes 786440 | tf_op jit(solution)/shard_map/ppermute | solution.py:12
  121.1 3.8 %fusion.26 = f32[2,512,512]{2,1,0:T(8,128)} fusion(f32[2,1,512,512]{2,3,0,1:T(8,128)S(1)} %bitcast_divide_fusion.3, f32[2,1,512,512]{3,2,0,1:T(8,128)} %copy.79), kind=kOutput, calls=%fused_computation.41 | convolution fusion | flops 538968064 | bytes 6291456 | tf_op jit(solution)/shard_map/ijac,ijbc->iab/dot_general | solution.py:51
  124.9 0.6 collective-permute-done.6
  125.5 0.5 bitcast_divide_fusion.1
  126.0 1.8 %copy.85 = f32[2,1,512,512]{3,2,0,1:T(8,128)} copy(f32[2,1,512,512]{2,3,0,1:T(8,128)S(1)} %bitcast_divide_fusion.1) | data formatting | bytes 4194304 | tf_op jit(solution)/shard_map/div | solution.py:48
  127.8 3.9 %fusion.32 = f32[2,512,512]{2,1,0:T(8,128)} fusion(f32[2,1,512,512]{2,3,0,1:T(8,128)S(1)} %bitcast_divide_fusion.1, f32[2,1,512,512]{3,2,0,1:T(8,128)} %copy.85), kind=kOutput, calls=%fused_computation.45 | convolution fusion | flops 538968064 | bytes 6291456 | tf_op jit(solution)/shard_map/ijac,ijbc->iab/dot_general | solution.py:51
  132.2 1.8 %copy.88 = f32[2,1,512,512]{3,2,0,1:T(8,128)} copy(f32[2,1,512,512]{2,3,0,1:T(8,128)S(1)} %bitcast_divide_fusion) | data formatting | bytes 4194304 | tf_op jit(solution)/shard_map/div | solution.py:48
  134.1 9.5 %add_add_fusion = f32[2,512,512]{2,1,0:T(8,128)} fusion(f32[2,512,512]{2,1,0:T(8,128)} %fusion.32, f32[2,512,512]{2,1,0:T(8,128)} %fusion.29, f32[2,512,512]{2,1,0:T(8,128)} %fusion.26, f32[2,512,512]{2,1,0:T(8,128)} %fusion.23, f32[2,512,512]{2,1,0:T(8,128)} %fusion.20, f32[2,512,512]{2,1,0:T(8,128)} %fusion.17, f32[2,512,512]{2,1,0:T(8,128)} %fusion.11, ...), kind=kOutput, calls=%fused_computation.27 | convolution fusion | flops 543162368 | bytes 23068672 | tf_op jit(solution)/shard_map/ijac,ijbc->iab/dot_general | solution.py:51
  143.5 12.2 %reduce-scatter.5.cloned.1.call-done = f32[2,256,512]{2,1,0:T(8,128)} async-done(((f32[2,512,512]{2,1,0:T(8,128)}), f32[2,256,512]{2,1,0:T(8,128)}) %reduce-scatter.5.cloned.1.call-update) | async-done | bytes 1048592 | tf_op jit(solution)/shard_map/reduce_scatter | solution.py:66
  (39 shorter events, 2.1 us)
Async XLA Ops:
  6.5 1.0 copy-start
  6.5 9.0 %copy-start.10 = (f32[32]{0:T(128)S(1)}, f32[32]{0:T(128)}, u32[]{:S(2)}) copy-start(f32[32]{0:T(128)} %param.8) | copy-start | bytes 388
  6.5 20.1 %reduce-scatter.3.cloned.1.call-start = ((), (), s32[]{:S(2)}) async-start(), calls=%async_computation.3 | async-start | bytes 1572864 | tf_op jit(solution)/shard_map/reduce_scatter | solution.py:26
  15.3 25.8 %copy-start.11 = (f32[512]{0:T(512)S(1)}, f32[512]{0:T(512)}, u32[]{:S(2)}) copy-start(f32[512]{0:T(512)} %param.9) | copy-start | bytes 6148
  28.6 17.1 %all-to-all-start = ((bf16[16,32,256]{2,0,1:T(8,128)(2,1)}), bf16[16,32,256]{2,0,1:T(8,128)(2,1)S(1)}, u32[]{:S(2)}, u32[]{:S(2)}) async-start(bf16[16,32,256]{2,0,1:T(8,128)(2,1)} %copy.61), calls=%async_computation.1 | async-start | bytes 524288 | tf_op jit(solution)/shard_map/all_to_all | solution.py:29
  35.4 120.4 %reduce-scatter.5.cloned.1.call-start = ((), (), s32[]{:S(2)}) async-start(), calls=%async_computation.4 | async-start | bytes 3145728 | tf_op jit(solution)/shard_map/reduce_scatter | solution.py:66
  47.9 20.6 %collective-permute-start = (bf16[256,1,512]{2,0,1:T(8,128)(2,1)S(1)}, bf16[256,1,512]{2,0,1:T(8,128)(2,1)S(1)}, u32[]{:S(2)}, u32[]{:S(2)}) collective-permute-start(bf16[256,1,512]{2,0,1:T(8,128)(2,1)S(1)} %constant_dynamic-slice_fusion), channel_id=1, source_target_pairs={{30,0},{0,2},{2,4},{4,6},{6,8},{8,10},{10,12},{12,14},{14,16},{16,... | collective-permute-start | bytes 786440 | tf_op jit(solution)/shard_map/ppermute | solution.py:12
  48.7 13.5 %collective-permute-start.1 = (bf16[256,1,512]{2,0,1:T(8,128)(2,1)S(1)}, bf16[256,1,512]{2,0,1:T(8,128)(2,1)S(1)}, u32[]{:S(2)}, u32[]{:S(2)}) collective-permute-start(bf16[256,1,512]{2,0,1:T(8,128)(2,1)S(1)} %constant_dynamic-slice_fusion), channel_id=1, source_target_pairs={{2,0},{4,2},{6,4},{8,6},{10,8},{12,10},{14,12},{16,14},{18,16},{20... | collective-permute-start | bytes 786440 | tf_op jit(solution)/shard_map/ppermute | solution.py:12
  57.1 5.2 %copy-start.2 = (f32[512,512]{0,1:T(8,128)S(1)}, f32[512,512]{0,1:T(8,128)}, u32[]{:S(2)}) copy-start(f32[512,512]{0,1:T(8,128)} %broadcast_add_fusion) | copy-start | bytes 3145732
  64.6 3.9 %copy-start.3 = (f32[512,512]{0,1:T(8,128)S(1)}, f32[512,512]{0,1:T(8,128)}, u32[]{:S(2)}) copy-start(f32[512,512]{0,1:T(8,128)} %broadcast_add_fusion) | copy-start | bytes 3145732
  70.9 14.9 %copy-start.4 = (f32[512,512]{0,1:T(8,128)S(1)}, f32[512,512]{0,1:T(8,128)}, u32[]{:S(2)}) copy-start(f32[512,512]{0,1:T(8,128)} %broadcast_add_fusion) | copy-start | bytes 3145732
  70.9 21.3 %collective-permute-start.2 = (bf16[256,1,512]{2,0,1:T(8,128)(2,1)S(1)}, bf16[256,1,512]{2,0,1:T(8,128)(2,1)S(1)}, u32[]{:S(2)}, u32[]{:S(2)}) collective-permute-start(bf16[256,1,512]{2,0,1:T(8,128)(2,1)S(1)} %collective-permute-done), channel_id=1, source_target_pairs={{30,0},{0,2},{2,4},{4,6},{6,8},{8,10},{10,12},{12,14},{14,16},{16,... | collective-permute-start | bytes 786440 | tf_op jit(solution)/shard_map/ppermute | solution.py:12
  71.5 13.6 %collective-permute-start.3 = (bf16[256,1,512]{2,0,1:T(8,128)(2,1)S(1)}, bf16[256,1,512]{2,0,1:T(8,128)(2,1)S(1)}, u32[]{:S(2)}, u32[]{:S(2)}) collective-permute-start(bf16[256,1,512]{2,0,1:T(8,128)(2,1)S(1)} %collective-permute-done.1), channel_id=1, source_target_pairs={{2,0},{4,2},{6,4},{8,6},{10,8},{12,10},{14,12},{16,14},{18,16},{20... | collective-permute-start | bytes 786440 | tf_op jit(solution)/shard_map/ppermute | solution.py:12
  85.1 0.7 copy-start.12
  88.2 4.0 %copy-start.5 = (f32[512,512]{0,1:T(8,128)S(1)}, f32[512,512]{0,1:T(8,128)}, u32[]{:S(2)}) copy-start(f32[512,512]{0,1:T(8,128)} %broadcast_add_fusion) | copy-start | bytes 3145732
  94.5 12.4 %copy-start.6 = (f32[512,512]{0,1:T(8,128)S(1)}, f32[512,512]{0,1:T(8,128)}, u32[]{:S(2)}) copy-start(f32[512,512]{0,1:T(8,128)} %broadcast_add_fusion) | copy-start | bytes 3145732
  94.5 18.7 %collective-permute-start.4 = (bf16[256,1,512]{2,0,1:T(8,128)(2,1)S(1)}, bf16[256,1,512]{2,0,1:T(8,128)(2,1)S(1)}, u32[]{:S(2)}, u32[]{:S(2)}) collective-permute-start(bf16[256,1,512]{2,0,1:T(8,128)(2,1)S(1)} %collective-permute-done.2), channel_id=1, source_target_pairs={{30,0},{0,2},{2,4},{4,6},{6,8},{8,10},{10,12},{12,14},{14,16},{16,... | collective-permute-start | bytes 786440 | tf_op jit(solution)/shard_map/ppermute | solution.py:12
  94.8 12.1 %collective-permute-start.5 = (bf16[256,1,512]{2,0,1:T(8,128)(2,1)}, bf16[256,1,512]{2,0,1:T(8,128)(2,1)S(1)}, u32[]{:S(2)}, u32[]{:S(2)}) collective-permute-start(bf16[256,1,512]{2,0,1:T(8,128)(2,1)} %copy-done.12), channel_id=1, source_target_pairs={{2,0},{4,2},{6,4},{8,6},{10,8},{12,10},{14,12},{16,14},{18,16},{20... | collective-permute-start | bytes 786440 | tf_op jit(solution)/shard_map/ppermute | solution.py:12
  109.2 3.9 %copy-start.7 = (f32[512,512]{0,1:T(8,128)S(1)}, f32[512,512]{0,1:T(8,128)}, u32[]{:S(2)}) copy-start(f32[512,512]{0,1:T(8,128)} %broadcast_add_fusion) | copy-start | bytes 3145732
  115.5 10.1 %copy-start.8 = (f32[512,512]{0,1:T(8,128)S(1)}, f32[512,512]{0,1:T(8,128)}, u32[]{:S(2)}) copy-start(f32[512,512]{0,1:T(8,128)} %broadcast_add_fusion) | copy-start | bytes 3145732
  115.5 10.1 %collective-permute-start.6 = (bf16[256,1,512]{2,0,1:T(8,128)(2,1)S(1)}, bf16[256,1,512]{2,0,1:T(8,128)(2,1)S(1)}, u32[]{:S(2)}, u32[]{:S(2)}) collective-permute-start(bf16[256,1,512]{2,0,1:T(8,128)(2,1)S(1)} %collective-permute-done.4), channel_id=1, source_target_pairs={{30,0},{0,2},{2,4},{4,6},{6,8},{8,10},{10,12},{12,14},{14,16},{16,... | collective-permute-start | bytes 786440 | tf_op jit(solution)/shard_map/ppermute | solution.py:12
  115.8 16.0 %collective-permute-start.7 = (bf16[256,1,512]{2,0,1:T(8,128)(2,1)S(1)}, bf16[256,1,512]{2,0,1:T(8,128)(2,1)S(1)}, u32[]{:S(2)}, u32[]{:S(2)}) collective-permute-start(bf16[256,1,512]{2,0,1:T(8,128)(2,1)S(1)} %collective-permute-done.5), channel_id=1, source_target_pairs={{2,0},{4,2},{6,4},{8,6},{10,8},{12,10},{14,12},{16,14},{18,16},{20... | collective-permute-start | bytes 786440 | tf_op jit(solution)/shard_map/ppermute | solution.py:12
  127.8 3.9 %copy-start.9 = (f32[512,512]{0,1:T(8,128)S(1)}, f32[512,512]{0,1:T(8,128)}, u32[]{:S(2)}) copy-start(f32[512,512]{0,1:T(8,128)} %broadcast_add_fusion) | copy-start | bytes 3145732
  134.1 21.7 %copy-start.1 = (bf16[384,512]{1,0:T(8,128)(2,1)S(1)}, bf16[384,512]{1,0:T(8,128)(2,1)}, u32[]{:S(2)}) copy-start(bf16[384,512]{1,0:T(8,128)(2,1)} %param.7) | copy-start | bytes 1179652
Sparse Core Ops, SparseCore 0:
  15.5 11.1 reduce-scatter.2
  143.7 12.0 reduce-scatter.4
where the time goes:
time: 163 us
  matrix products  53.9 us (33%)
  waiting for transfers between devices  35.7 us (22%)
  starting transfers between devices  29.4 us (18%)
  local copies, waits for them, and re-layouts  19.9 us (12%)
  between operations  13.7 us (8%)
  other arithmetic  7.87 us (5%)
  blocking collectives  2.18 us (1%)
    dot_general x9, matrix products, add_pairs(): jnp.einsum('ijac,ijbc->iab', amplitude, mixed, preferred_element_type=jnp...  40.7 us
    ppermute x8, starting transfers between devices, passed_along(): return lax.ppermute(block, axis, route)  22.5 us
    div x9, local copies, waits for them, and re-layouts, add_pairs(): scaled = integrals / energy_gap  16.6 us
    reduce_scatter x1, waiting for transfers between devices, shards(): return lax.psum_scatter(density_sum, 'ao', scatter_dimension=1, tiled=True)  12.2 us
    reduce_scatter x1, waiting for transfers between devices, shards(): lax.psum_scatter(partial_sum, 'ao', scatter_dimension=2, tiled=True)  10.4 us
    ppermute x8, waiting for transfers between devices, passed_along(): return lax.ppermute(block, axis, route)  9.53 us
    dot_general x1, matrix products, shards(): jnp.einsum('qmi,ma->qia', half_ints, vir_coef, preferred_element_type=jnp...  7.81 us
    all_to_all x1, starting transfers between devices, shards(): lax.all_to_all(summed_half, 'aux', split_axis=1, concat_axis=0, tiled=True)  6.77 us
  transfers between devices with their start and end apart: 11, of which 7 were waited for; matrix products, arithmetic and copies ran while one was open for 32% of the time, Pallas kernels for 0%

commit v1 on v0

v1 whole, which is shorter than its diff:
```python
import functools

import jax
import jax.numpy as jnp
from jax import lax
from jax.experimental import pallas as pl
from jax.experimental.pallas import tpu as pltpu
from jax.sharding import PartitionSpec as P

CYCLE = 4
MESH = pl.DeviceIdType.MESH
NT = (((1,), (1,)), ((), ()))


def offset_of(slot):
    size = CYCLE + 1 - (slot + 1) // 2
    return 0 if slot == 0 else (size if slot % 2 else -size)


def pairs_kernel(
    aux_count, share, own_ref, occ_ref, vir_row_ref, vir_col_ref, out_ref,
    slots, own_t, vis_t, vir_pairs, amp, mix, acc, outgoing, incoming,
    send_sems, recv_sems, swap_sems,
):
    me = lax.axis_index("aux")
    core = lax.axis_index("ao")
    other = 1 - core
    block, _, nvir = own_ref.shape
    half = nvir // 2
    slot_count = 2 * CYCLE + 1

    barrier = pltpu.get_barrier_semaphore()
    for slot in range(1, slot_count):
        target = lax.rem(me + aux_count + offset_of(slot), aux_count)
        pl.semaphore_signal(barrier, inc=1, device_id=(target, core), device_id_type=MESH)
    pl.semaphore_signal(barrier, inc=1, device_id=(me, other), device_id_type=MESH)
    pl.semaphore_wait(barrier, slot_count)

    piece = own_ref.at[pl.ds(core * share, share)]
    sends = []
    for slot in range(1, slot_count):
        target = lax.rem(me + aux_count - offset_of(slot), aux_count)
        sends.append(
            pltpu.make_async_remote_copy(
                src_ref=piece,
                dst_ref=slots.at[slot],
                send_sem=send_sems.at[slot],
                recv_sem=recv_sems.at[slot],
                device_id=(target, core),
                device_id_type=MESH,
            )
        )
        sends[-1].start()
    pltpu.make_async_copy(piece, slots.at[0], recv_sems.at[0]).start()

    for i in range(block):
        own_t[i] = own_ref[i].T
    vir_pairs[...] = vir_col_ref[...] + vir_row_ref[...]
    acc[...] = jnp.zeros_like(acc)

    def visit(slot, carry):
        size = CYCLE + 1 - lax.div(slot + 1, 2)
        signed = jnp.where(lax.rem(slot, 2) == 1, size, -size)
        offset = jnp.where(slot == 0, 0, signed)
        owner = lax.rem(me + aux_count + offset, aux_count)
        pltpu.make_async_copy(slots.at[slot], slots.at[slot], recv_sems.at[slot]).wait()
        for s in range(share):
            pair_energy = occ_ref[owner * block + core * share + s]
            visitor = slots[slot, s]
            vis_t[...] = visitor.T
            for i in range(block):
                energy = occ_ref[me * block + i] + pair_energy
                for t in range(2):
                    rows = slice(t * half, (t + 1) * half)
                    direct = jnp.dot(own_t[i, rows], visitor, preferred_element_type=jnp.float32)
                    swapped = jnp.dot(vis_t[rows], own_ref[i], preferred_element_type=jnp.float32)
                    inverse = 1.0 / (energy - vir_pairs[rows])
                    amp[i, rows] = (direct * inverse).astype(jnp.bfloat16)
                    mix[i, rows] = ((2.0 * direct - swapped) * inverse).astype(jnp.bfloat16)
                acc[i] += lax.dot_general(amp[i], mix[i], NT, preferred_element_type=jnp.float32)
        return carry

    lax.fori_loop(0, slot_count, visit, 0)

    outgoing[...] = acc[:, pl.ds(pl.multiple_of(other * half, half), half)].astype(jnp.bfloat16)
    swap = pltpu.make_async_remote_copy(
        src_ref=outgoing,
        dst_ref=incoming,
        send_sem=swap_sems.at[0],
        recv_sem=swap_sems.at[1],
        device_id=(me, other),
        device_id_type=MESH,
    )
    swap.start()
    for send in sends:
        send.wait_send()
    swap.wait()
    kept = acc[:, pl.ds(pl.multiple_of(core * half, half), half)]
    out_ref[...] = kept + incoming[...].astype(jnp.float32)


def pair_densities(own_block, occ_energy, vir_energy, aux_count, share):
    block, naux, nvir = own_block.shape
    half = nvir // 2
    slot_count = 2 * CYCLE + 1
    vmem = pl.BlockSpec(memory_space=pltpu.VMEM)
    return pl.pallas_call(
        functools.partial(pairs_kernel, aux_count, share),
        out_shape=jax.ShapeDtypeStruct((block, half, nvir), jnp.float32),
        in_specs=[vmem, pl.BlockSpec(memory_space=pltpu.SMEM), vmem, vmem],
        out_specs=vmem,
        scratch_shapes=[
            pltpu.VMEM((slot_count, share, naux, nvir), jnp.bfloat16),
            pltpu.VMEM((block, nvir, naux), jnp.bfloat16),
            pltpu.VMEM((nvir, naux), jnp.bfloat16),
            pltpu.VMEM((nvir, nvir), jnp.float32),
            pltpu.VMEM((block, nvir, nvir), jnp.bfloat16),
            pltpu.VMEM((block, nvir, nvir), jnp.bfloat16),
            pltpu.VMEM((block, nvir, nvir), jnp.float32),
            pltpu.VMEM((block, half, nvir), jnp.bfloat16),
            pltpu.VMEM((block, half, nvir), jnp.bfloat16),
            pltpu.SemaphoreType.DMA((slot_count,)),
            pltpu.SemaphoreType.DMA((slot_count,)),
            pltpu.SemaphoreType.DMA((2,)),
        ],
        compiler_params=pltpu.CompilerParams(collective_id=0, has_side_effects=True, vmem_limit_bytes=48 * 2**20),
    )(own_block, occ_energy, vir_energy[None, :], vir_energy[:, None])


def shards(ints, occ_coef, vir_coef, occ_energy, vir_energy):
    core = lax.axis_index("ao")
    aux_count = lax.axis_size("aux")
    ao_count = lax.axis_size("ao")
    share = occ_coef.shape[1] // aux_count // ao_count
    half = vir_coef.shape[1] // ao_count
    half_ints = jnp.einsum(
        "qmn,ni->qmi", ints, occ_coef, preferred_element_type=jnp.float32
    ).astype(jnp.bfloat16)
    partial_sum = jnp.einsum("qmi,ma->qia", half_ints, vir_coef, preferred_element_type=jnp.float32)
    given = lax.dynamic_slice_in_dim(partial_sum, (1 - core) * half, half, 2).astype(jnp.bfloat16)
    taken = lax.ppermute(given, "ao", [(0, 1), (1, 0)])
    kept = lax.dynamic_slice_in_dim(partial_sum, core * half, half, 2)
    summed = (kept + taken.astype(jnp.float32)).astype(jnp.bfloat16)
    grouped = lax.all_to_all(summed, "aux", split_axis=1, concat_axis=0, tiled=True)
    own_block = lax.all_gather(grouped, "ao", axis=2, tiled=True)
    return pair_densities(
        jnp.swapaxes(own_block, 0, 1), occ_energy, vir_energy, aux_count, share
    )


def solution(mesh):
    return jax.shard_map(
        shards,
        mesh=mesh,
        in_specs=(P("aux", "ao", None), P(), P("ao", None), P(), P()),
        out_specs=P("aux", "ao", None),
        check_vma=False,
    )
```

time: 163 us -> 79.4 us (0.49)
  matrix products: 53.9 us -> 6.84 us
  Pallas kernels: 0 us -> 47 us
  waiting for transfers between devices: 35.7 us -> 11.2 us
  starting transfers between devices: 29.4 us -> 8.78 us
  local copies, waits for them, and re-layouts: 19.9 us -> 3.03 us
  between operations: 13.7 us -> 0.06 us
  other arithmetic: 7.87 us -> 0.1 us
    pallas_call x0 -> x1, Pallas kernels: none -> 47 us  [pair_densities(): pl.pallas_call(functools.partial(pairs_kernel, aux_count, share), out_sha...]
    dot_general x18 -> x0, matrix products: 46.1 us -> none  [the longest x9 40.7 us: add_pairs(): jnp.einsum('ijac,ijbc->iab', amplitude, mixed, preferred_element_type=jnp...]
    reduce_scatter x2 -> x0, waiting for transfers between devices: 22.7 us -> none  [the longest x1 12.2 us: shards(): return lax.psum_scatter(density_sum, 'ao', scatter_dimension=1, tiled=True)]
    ppermute x8 -> x1, starting transfers between devices: 22.5 us -> 0.56 us  [shards(): taken = lax.ppermute(given, 'ao', [(0, 1), (1, 0)])]
    div x9 -> x0, local copies, waits for them, and re-layouts: 16.6 us -> none  [add_pairs(): scaled = integrals / energy_gap]
    ppermute x8 -> x1, waiting for transfers between devices: 9.53 us -> 1.16 us  [shards(): taken = lax.ppermute(given, 'ao', [(0, 1), (1, 0)])]
    add x3 -> x0, other arithmetic: 6.8 us -> none  [the longest x2 5.69 us: add_pairs(): own_energy[:, None, None, None] + pair_energy[None, :, None, None]]
    all_to_all x1, waiting for transfers between devices: 3.48 us -> 10 us  [shards(): lax.all_to_all(summed, 'aux', split_axis=1, concat_axis=0, tiled=True)]
  transfers between devices with their start and end apart: 11 -> 2, of which waited for: 7 -> 2; matrix products, arithmetic and copies ran while one was open for 32% -> 0% of each run, Pallas kernels for 0% -> 0%
where the time goes in v1:
time: 79.4 us; the launch traced here: 79.2 us
  Pallas kernels  47 us (59%)
  waiting for transfers between devices  11.2 us (14%)
  starting transfers between devices  8.78 us (11%)
  matrix products  6.84 us (9%)
  local copies, waits for them, and re-layouts  3.03 us (4%)
  blocking collectives  2.18 us (3%)
    pallas_call x1, Pallas kernels, pair_densities(): pl.pallas_call(functools.partial(pairs_kernel, aux_count, share), out_sha...  47 us
    all_to_all x1, waiting for transfers between devices, shards(): lax.all_to_all(summed, 'aux', split_axis=1, concat_axis=0, tiled=True)  10 us
    all_to_all x1, starting transfers between devices, shards(): lax.all_to_all(summed, 'aux', split_axis=1, concat_axis=0, tiled=True)  8.22 us
    dot_general x1, matrix products, shards(): jnp.einsum('qmi,ma->qia', half_ints, vir_coef, preferred_element_type=jnp...  6.84 us
    all_gather x1, blocking collectives, shards(): own_block = lax.all_gather(grouped, 'ao', axis=2, tiled=True)  2.18 us
    unnamed x7, local copies, waits for them, and re-layouts  1.97 us
  transfers between devices with their start and end apart: 2, of which 2 were waited for; matrix products, arithmetic and copies ran while one was open for 0% of the time, Pallas kernels for 0%

profile of v1, /device:TPU:0, one launch (start us, length us, event | category | flops | bytes accessed | tf_op | source)
XLA Modules:
  0.0 79.2 jit_solution(78880973750580334)
XLA Ops:
  0.0 0.0 copy-start
  0.0 0.0 copy-start.1
  0.0 0.0 copy-start.2
  0.0 1.0 %copy-done = bf16[384,512]{1,0:T(8,128)(2,1)S(1)} copy-done((bf16[384,512]{1,0:T(8,128)(2,1)S(1)}, bf16[384,512]{1,0:T(8,128)(2,1)}, u32[]{:S(2)}) %copy-start) | copy-done | bytes 393240
  1.0 6.8 %fusion = f32[16,32,512]{2,1,0:T(8,128)S(1)} fusion(bf16[16,384,768]{2,1,0:T(8,128)(2,1)} %param.5, bf16[384,512]{1,0:T(8,128)(2,1)S(1)} %copy-done, bf16[768,32]{0,1:T(8,128)(2,1)} %param.6), kind=kOutput, calls=%fused_computation.1 | convolution fusion | flops 503513088 | bytes 10928128 | tf_op jit(solution)/shard_map/qmi,ma->qia/dot_general | solution.py:139
  7.9 0.6 collective-permute-start
  8.5 1.2 %collective-permute-done = bf16[16,32,256]{2,1,0:T(8,128)(2,1)S(1)} collective-permute-done((bf16[16,32,256]{2,1,0:T(8,128)(2,1)S(1)}, bf16[16,32,256]{2,1,0:T(8,128)(2,1)S(1)}, u32[]{:S(2)}, u32[]{:S(2)}) %collective-permute-start) | collective-permute-done | bytes 262176 | tf_op jit(solution)/shard_map/ppermute | solution.py:141
  9.6 0.1 add_convert_fusion
  9.7 0.9 %copy.9 = bf16[16,32,256]{2,0,1:T(8,128)(2,1)} copy(bf16[16,32,256]{2,1,0:T(8,128)(2,1)S(1)} %add_convert_fusion) | data formatting | bytes 524288 | tf_op jit(solution)/shard_map/convert_element_type | solution.py:143
  10.6 8.2 %all-to-all-start = ((bf16[16,32,256]{2,0,1:T(8,128)(2,1)}), bf16[16,32,256]{2,0,1:T(8,128)(2,1)S(1)}, u32[]{:S(2)}, u32[]{:S(2)}) async-start(bf16[16,32,256]{2,0,1:T(8,128)(2,1)} %copy.9), calls=%async_computation | async-start | bytes 524288 | tf_op jit(solution)/shard_map/all_to_all | solution.py:144
  18.8 0.0 copy-done.1
  18.8 0.1 copy.11.vir_col_ref
  19.0 10.0 %all-to-all-done = bf16[16,32,256]{2,0,1:T(8,128)(2,1)S(1)} async-done(((bf16[16,32,256]{2,0,1:T(8,128)(2,1)}), bf16[16,32,256]{2,0,1:T(8,128)(2,1)S(1)}, u32[]{:S(2)}, u32[]{:S(2)}) %all-to-all-start) | async-done | bytes 262176 | tf_op jit(solution)/shard_map/all_to_all | solution.py:144
  29.0 2.2 %all_gather.3 = bf16[256,2,512]{2,0,1:T(8,128)(2,1)S(1)} all-gather(bf16[256,2,256]{2,0,1:T(8,128)(2,1)S(1)} %bitcast.18), channel_id=1, replica_groups=mesh['aux'=16,'ao'=2] {'ao'}, dimensions={2}, use_global_device_ids=true | all-gather | bytes 786432 | tf_op jit(solution)/shard_map/all_gather | solution.py:145
  31.2 0.0 copy-done.2
  31.2 47.0 %shard_map.55 = f32[2,256,512]{2,1,0:T(8,128)S(1)} custom-call(bf16[2,256,512]{2,1,0:T(8,128)(2,1)S(1)} %bitcast.15, f32[32]{0:T(128)S(1)} %copy-done.2, f32[1,512]{1,0:T(1,128)S(1)} %bitcast.17, f32[512,1]{1,0:T(8,128)S(1)} %copy.11.vir_col_ref), custom_call_target="tpu_custom_call" | custom-call | tf_op jit(solution)/shard_map/pallas_call | solution.py:107
  78.2 1.0 %copy.13 = f32[2,256,512]{2,1,0:T(8,128)} copy(f32[2,256,512]{2,1,0:T(8,128)S(1)} %shard_map.55) | data formatting | bytes 2097152
  (2 shorter events, 0.1 us)
Async XLA Ops:
  0.0 1.0 %copy-start = (bf16[384,512]{1,0:T(8,128)(2,1)S(1)}, bf16[384,512]{1,0:T(8,128)(2,1)}, u32[]{:S(2)}) copy-start(bf16[384,512]{1,0:T(8,128)(2,1)} %param.7) | copy-start | bytes 1179652
  0.0 18.8 %copy-start.1 = (f32[512]{0:T(512)S(1)}, f32[512]{0:T(512)}, u32[]{:S(2)}) copy-start(f32[512]{0:T(512)} %param.9) | copy-start | bytes 6148
  0.0 31.2 %copy-start.2 = (f32[32]{0:T(128)S(1)}, f32[32]{0:T(128)}, u32[]{:S(2)}) copy-start(f32[32]{0:T(128)} %occ_ref.1) | copy-start | bytes 388
  7.9 1.7 %collective-permute-start = (bf16[16,32,256]{2,1,0:T(8,128)(2,1)S(1)}, bf16[16,32,256]{2,1,0:T(8,128)(2,1)S(1)}, u32[]{:S(2)}, u32[]{:S(2)}) collective-permute-start(bf16[16,32,256]{2,1,0:T(8,128)(2,1)S(1)} %dynamic-slice_convert_fusion), channel_id=1, source_target_pairs={{0,1},{1,0},{2,3},{3,2},{4,5},{5,4},{6,7},{7,6},{8,9},{9,8},{10,11... | collective-permute-start | bytes 786440 | tf_op jit(solution)/shard_map/ppermute | solution.py:141
  10.6 18.4 %all-to-all-start = ((bf16[16,32,256]{2,0,1:T(8,128)(2,1)}), bf16[16,32,256]{2,0,1:T(8,128)(2,1)S(1)}, u32[]{:S(2)}, u32[]{:S(2)}) async-start(bf16[16,32,256]{2,0,1:T(8,128)(2,1)} %copy.9), calls=%async_computation | async-start | bytes 524288 | tf_op jit(solution)/shard_map/all_to_all | solution.py:144

commit v2 on v1

--- a/solution.py
+++ b/solution.py
@@ -18,9 +18,9 @@
 
 
 def pairs_kernel(
-    aux_count, share, own_ref, occ_ref, vir_row_ref, vir_col_ref, out_ref,
-    slots, own_t, vis_t, vir_pairs, amp, mix, acc, outgoing, incoming,
-    send_sems, recv_sems, swap_sems,
+    aux_count, ao_count, share, slab_ref, occ_ref, vir_row_ref, vir_col_ref, out_ref,
+    own_ref, slots, own_t, vis_t, vir_pairs, amp, mix, acc, outgoing, incoming,
+    spread_sems, gather_sems, send_sems, recv_sems, swap_sems,
 ):
     me = lax.axis_index("aux")
     core = lax.axis_index("ao")
@@ -28,13 +28,59 @@
     block, _, nvir = own_ref.shape
     half = nvir // 2
     slot_count = 2 * CYCLE + 1
+    total = aux_count * ao_count
+    rank = me * ao_count + core
+    slab_rows = slab_ref.shape[1]
+    slab_columns = slab_ref.shape[2]
+
+    def place_of(number):
+        aux, ao = lax.div(number, ao_count), lax.rem(number, ao_count)
+        rows = pl.ds(pl.multiple_of(aux * slab_rows, slab_rows), slab_rows)
+        columns = pl.ds(pl.multiple_of(ao * slab_columns, slab_columns), slab_columns)
+        return own_ref.at[:, rows, columns]
+
+    def spread(step):
+        number = lax.rem(rank + step, total)
+        aux, ao = lax.div(number, ao_count), lax.rem(number, ao_count)
+        return pltpu.make_async_remote_copy(
+            src_ref=slab_ref.at[pl.ds(aux * block, block)],
+            dst_ref=place_of(rank),
+            send_sem=spread_sems.at[step],
+            recv_sem=gather_sems.at[step],
+            device_id=(aux, ao),
+            device_id_type=MESH,
+        )
 
     barrier = pltpu.get_barrier_semaphore()
-    for slot in range(1, slot_count):
-        target = lax.rem(me + aux_count + offset_of(slot), aux_count)
-        pl.semaphore_signal(barrier, inc=1, device_id=(target, core), device_id_type=MESH)
-    pl.semaphore_signal(barrier, inc=1, device_id=(me, other), device_id_type=MESH)
-    pl.semaphore_wait(barrier, slot_count)
+
+    def greet(step, carry):
+        number = lax.rem(rank + step, total)
+        target = (lax.div(number, ao_count), lax.rem(number, ao_count))
+        pl.semaphore_signal(barrier, inc=1, device_id=target, device_id_type=MESH)
+        return carry
+
+    def start_spread(step, carry):
+        spread(step).start()
+        return carry
+
+    def end_spread(step, carry):
+        spread(step).wait_send()
+        return carry
+
+    def gather(step, carry):
+        place = place_of(lax.rem(rank + total - step, total))
+        pltpu.make_async_copy(place, place, gather_sems.at[step]).wait()
+        return carry
+
+    lax.fori_loop(1, total, greet, 0)
+    vir_pairs[...] = vir_col_ref[...] + vir_row_ref[...]
+    acc[...] = jnp.zeros_like(acc)
+    pl.semaphore_wait(barrier, total - 1)
+    lax.fori_loop(1, total, start_spread, 0)
+    pltpu.make_async_copy(
+        slab_ref.at[pl.ds(me * block, block)], place_of(rank), gather_sems.at[0]
+    ).start()
+    lax.fori_loop(0, total, gather, 0)
 
     piece = own_ref.at[pl.ds(core * share, share)]
     sends = []
@@ -55,8 +101,6 @@
 
     for i in range(block):
         own_t[i] = own_ref[i].T
-    vir_pairs[...] = vir_col_ref[...] + vir_row_ref[...]
-    acc[...] = jnp.zeros_like(acc)
 
     def visit(slot, carry):
         size = CYCLE + 1 - lax.div(slot + 1, 2)
@@ -94,22 +138,27 @@
     swap.start()
     for send in sends:
         send.wait_send()
+    lax.fori_loop(1, total, end_spread, 0)
     swap.wait()
     kept = acc[:, pl.ds(pl.multiple_of(core * half, half), half)]
     out_ref[...] = kept + incoming[...].astype(jnp.float32)
 
 
-def pair_densities(own_block, occ_energy, vir_energy, aux_count, share):
-    block, naux, nvir = own_block.shape
+def pair_densities(slab, occ_energy, vir_energy, aux_count, ao_count, share):
+    block = slab.shape[0] // aux_count
+    naux = slab.shape[1] * aux_count
+    nvir = slab.shape[2] * ao_count
+    total = aux_count * ao_count
     half = nvir // 2
     slot_count = 2 * CYCLE + 1
     vmem = pl.BlockSpec(memory_space=pltpu.VMEM)
     return pl.pallas_call(
-        functools.partial(pairs_kernel, aux_count, share),
+        functools.partial(pairs_kernel, aux_count, ao_count, share),
         out_shape=jax.ShapeDtypeStruct((block, half, nvir), jnp.float32),
         in_specs=[vmem, pl.BlockSpec(memory_space=pltpu.SMEM), vmem, vmem],
         out_specs=vmem,
         scratch_shapes=[
+            pltpu.VMEM((block, naux, nvir), jnp.bfloat16),
             pltpu.VMEM((slot_count, share, naux, nvir), jnp.bfloat16),
             pltpu.VMEM((block, nvir, naux), jnp.bfloat16),
             pltpu.VMEM((nvir, naux), jnp.bfloat16),
@@ -119,12 +168,14 @@
             pltpu.VMEM((block, nvir, nvir), jnp.float32),
             pltpu.VMEM((block, half, nvir), jnp.bfloat16),
             pltpu.VMEM((block, half, nvir), jnp.bfloat16),
+            pltpu.SemaphoreType.DMA((total,)),
+            pltpu.SemaphoreType.DMA((total,)),
             pltpu.SemaphoreType.DMA((slot_count,)),
             pltpu.SemaphoreType.DMA((slot_count,)),
             pltpu.SemaphoreType.DMA((2,)),
         ],
         compiler_params=pltpu.CompilerParams(collective_id=0, has_side_effects=True, vmem_limit_bytes=48 * 2**20),
-    )(own_block, occ_energy, vir_energy[None, :], vir_energy[:, None])
+    )(slab, occ_energy, vir_energy[None, :], vir_energy[:, None])
 
 
 def shards(ints, occ_coef, vir_coef, occ_energy, vir_energy):
@@ -141,10 +192,8 @@
     taken = lax.ppermute(given, "ao", [(0, 1), (1, 0)])
     kept = lax.dynamic_slice_in_dim(partial_sum, core * half, half, 2)
     summed = (kept + taken.astype(jnp.float32)).astype(jnp.bfloat16)
-    grouped = lax.all_to_all(summed, "aux", split_axis=1, concat_axis=0, tiled=True)
-    own_block = lax.all_gather(grouped, "ao", axis=2, tiled=True)
     return pair_densities(
-        jnp.swapaxes(own_block, 0, 1), occ_energy, vir_energy, aux_count, share
+        jnp.swapaxes(summed, 0, 1), occ_energy, vir_energy, aux_count, ao_count, share
     )
 
 

time: 79.4 us -> 83.2 us (1.048)
  Pallas kernels: 47 us -> 73.1 us
  waiting for transfers between devices: 11.2 us -> 1.01 us
  starting transfers between devices: 8.78 us -> 0.56 us
  blocking collectives: 2.18 us -> 0 us
  local copies, waits for them, and re-layouts: 3.03 us -> 1.18 us
    pallas_call x1, Pallas kernels: 47 us -> 73.1 us  [pair_densities(): pl.pallas_call(functools.partial(pairs_kernel, aux_count, ao_count, share...]
    all_to_all x1 -> x0, waiting for transfers between devices: 10 us -> none  [shards(): lax.all_to_all(summed, 'aux', split_axis=1, concat_axis=0, tiled=True)]
    all_to_all x1 -> x0, starting transfers between devices: 8.22 us -> none  [shards(): lax.all_to_all(summed, 'aux', split_axis=1, concat_axis=0, tiled=True)]
    dot_general x0 -> x1, matrix products: none -> 6.55 us  [shards(): jnp.einsum('qmn,ni->qmi', ints, occ_coef, preferred_element_type=jnp.floa...]
    dot_general x1, matrix products: 6.84 us -> 0.45 us  [shards(): jnp.einsum('qmi,ma->qia', half_ints, vir_coef, preferred_element_type=jnp...]
    all_gather x1 -> x0, blocking collectives: 2.18 us -> none  [shards(): own_block = lax.all_gather(grouped, 'ao', axis=2, tiled=True)]
    unnamed x7, local copies, waits for them, and re-layouts: 1.97 us -> 0.99 us
    convert_element_type x1 -> x0, local copies, waits for them, and re-layouts: 0.85 us -> none  [shards(): summed = (kept + taken.astype(jnp.float32)).astype(jnp.bfloat16)]
  transfers between devices with their start and end apart: 2 -> 1, of which waited for: 2 -> 1; matrix products, arithmetic and copies ran while one was open for 0% -> 0% of each run, Pallas kernels for 0% -> 0%
where the time goes in v2:
time: 83.2 us; the launch traced here: 83 us
  Pallas kernels  73.1 us (88%)
  matrix products  7 us (8%)
  local copies, waits for them, and re-layouts  1.18 us (1%)
  waiting for transfers between devices  1.01 us (1%)
    pallas_call x1, Pallas kernels, pair_densities(): pl.pallas_call(functools.partial(pairs_kernel, aux_count, ao_count, share...  73.1 us
    dot_general x1, matrix products, shards(): jnp.einsum('qmn,ni->qmi', ints, occ_coef, preferred_element_type=jnp.floa...  6.55 us
  transfers between devices with their start and end apart: 1, of which 1 were waited for; matrix products, arithmetic and copies ran while one was open for 0% of the time, Pallas kernels for 0%

profile of v2, /device:TPU:0, one launch (start us, length us, event | category | flops | bytes accessed | tf_op | source)
XLA Modules:
  0.0 83.0 jit_solution(13680580362842859882)
XLA Ops:
  0.0 0.0 copy-start
  0.0 0.0 copy-start.1
  0.0 0.0 copy-start.2
  0.0 6.6 %convolution_convert_fusion = bf16[16,384,32]{1,2,0:T(8,128)(2,1)S(1)} fusion(bf16[16,384,768]{2,1,0:T(8,128)(2,1)} %param.5, bf16[768,32]{0,1:T(8,128)(2,1)} %param.6), kind=kOutput, calls=%fused_computation | convolution fusion | flops 302186496 | bytes 9879552 | tf_op jit(solution)/shard_map/qmn,ni->qmi/dot_general | solution.py:187
  6.6 0.0 copy-done
  6.6 0.4 fusion
  7.1 0.6 collective-permute-start
  7.6 0.0 copy-done.1
  7.7 0.1 copy.10.vir_col_ref
  7.8 1.0 %collective-permute-done = bf16[16,32,256]{2,0,1:T(8,128)(2,1)S(1)} collective-permute-done((bf16[16,32,256]{2,0,1:T(8,128)(2,1)S(1)}, bf16[16,32,256]{2,0,1:T(8,128)(2,1)S(1)}, u32[]{:S(2)}, u32[]{:S(2)}) %collective-permute-start) | collective-permute-done | bytes 262176 | tf_op jit(solution)/shard_map/ppermute | solution.py:192
  8.8 0.1 fusion.3.slab_ref
  8.9 0.0 copy-done.2
  8.9 73.1 %shard_map.55 = f32[2,256,512]{2,1,0:T(8,128)S(1)} custom-call(bf16[32,16,256]{2,1,0:T(8,128)(2,1)S(1)} %fusion.3.slab_ref, f32[32]{0:T(128)S(1)} %copy-done.2, f32[1,512]{1,0:T(1,128)S(1)} %bitcast.12, f32[512,1]{1,0:T(8,128)S(1)} %copy.10.vir_col_ref), custom_call_target="tpu_custom_call" | custom-call | tf_op jit(solution)/shard_map/pallas_call | solution.py:155
  82.0 1.0 %copy.16 = f32[2,256,512]{2,1,0:T(8,128)} copy(f32[2,256,512]{2,1,0:T(8,128)S(1)} %shard_map.55) | data formatting | bytes 2097152
  (1 shorter events, 0.0 us)
Async XLA Ops:
  0.0 6.6 %copy-start = (bf16[384,512]{1,0:T(8,128)(2,1)S(1)}, bf16[384,512]{1,0:T(8,128)(2,1)}, u32[]{:S(2)}) copy-start(bf16[384,512]{1,0:T(8,128)(2,1)} %param.7) | copy-start | bytes 1179652
  0.0 7.6 %copy-start.1 = (f32[512]{0:T(512)S(1)}, f32[512]{0:T(512)}, u32[]{:S(2)}) copy-start(f32[512]{0:T(512)} %param.9) | copy-start | bytes 6148
  0.0 8.9 %copy-start.2 = (f32[32]{0:T(128)S(1)}, f32[32]{0:T(128)}, u32[]{:S(2)}) copy-start(f32[32]{0:T(128)} %occ_ref.1) | copy-start | bytes 388
  7.1 1.7 %collective-permute-start = (bf16[16,32,256]{2,0,1:T(8,128)(2,1)S(1)}, bf16[16,32,256]{2,0,1:T(8,128)(2,1)S(1)}, u32[]{:S(2)}, u32[]{:S(2)}) collective-permute-start(bf16[16,32,256]{2,0,1:T(8,128)(2,1)S(1)} %dynamic-slice_convert_fusion), channel_id=1, source_target_pairs={{0,1},{1,0},{2,3},{3,2},{4,5},{5,4},{6,7},{7,6},{8,9},{9,8},{10,11... | collective-permute-start | bytes 786440 | tf_op jit(solution)/shard_map/ppermute | solution.py:192
